TPU v7x, 8 devices: a whole 2x2x1 slice. The times are simulated.
8 devices in a mesh: rep: 1 (over z), tp: 2 (over y), dp: 4 (over x, core).
Axes of the slice: x: 2, y: 2, z: 1, core: 2. Of those that a mesh axis runs over, the one named last changes fastest.
Arguments:
- x: bfloat16 [512, 2560], P(('rep', 'dp'))
- lengths: int32 [512], P(('rep', 'dp'))
- cache0: bfloat16 [512, 256, 288], P(('rep', 'dp'))
- cache1: bfloat16 [512, 256, 288], P(('rep', 'dp'))
- attn_gain: float32 [2, 2560], replicated
- kv_gain: float32 [2, 256], replicated
- q_gain: float32 [2, 768], replicated
- ffn_gain: float32 [2, 2560], replicated
- w_dkv: bfloat16 [2, 2560, 288], replicated
- w_qa: bfloat16 [2, 2560, 768], replicated
- w_qb: bfloat16 [2, 768, 3840], P(None, None, 'tp')
- w_uk: bfloat16 [2, 40, 64, 256], P(None, 'tp')
- w_uv: bfloat16 [2, 40, 256, 64], P(None, 'tp')
- w_o: bfloat16 [2, 2560, 2560], P(None, 'tp')
- w_gate: bfloat16 [2, 2560, 6400], replicated
- w_up: bfloat16 [2, 2560, 6400], replicated
- w_down: bfloat16 [2, 6400, 2560], replicated
Outputs:
- output 1: bfloat16 [512, 2560], P(('rep', 'dp'))
- output 2: bfloat16 [512, 256, 288], P(('rep', 'dp'))
- output 3: bfloat16 [512, 256, 288], P(('rep', 'dp'))
All inputs are finite; a program needn't handle non-finite values.
Results may differ from a plain program's by a relative error of at most 0.014556.
Values are sent between devices in bfloat16 or wider.
A program may use at most 1.25 GiB of HBM per device.

v0:
```python
import functools

import jax
import jax.numpy as jnp
from jax import lax
from jax.experimental import pallas as pl
from jax.experimental.pallas import tpu as pltpu
from jax.sharding import PartitionSpec as P

NORM_EPS = 1e-6
ROPE_BASE = 10000.0
F32 = jnp.float32
BF16 = jnp.bfloat16
ROWS_PER_STEP = 8
SLOTS = 12
AHEAD = 8
LANES = 128
PITCH_PAD = 8
HIDDEN_BLOCKS = 5
HIDDEN_SLOTS = 3
OUT_BLOCKS = 5
MESH = pl.DeviceIdType.MESH
VMEM_LIMIT = 60 * 1024 * 1024


def rms_norm(values, gain_vec):
    wide_vals = values.astype(F32)
    inv_rms = lax.rsqrt(jnp.mean(wide_vals * wide_vals, axis=-1, keepdims=True) + NORM_EPS)
    return (wide_vals * inv_rms * gain_vec).astype(BF16)


def rope_tables(lengths, rope_dim):
    half_dim = rope_dim // 2
    inv_freq = ROPE_BASE ** (-2.0 * jnp.arange(half_dim).astype(F32) / rope_dim)
    angles = lengths.astype(F32)[:, None] * inv_freq[None, :]
    cos_tab, sin_tab = jnp.cos(angles), jnp.sin(angles)
    return jnp.concatenate([cos_tab, cos_tab], axis=1), jnp.concatenate([-sin_tab, sin_tab], axis=1)


def rotate(turn, cos2, sin2):
    half = turn.shape[1] // 2
    swapped = jnp.concatenate([turn[:, half:], turn[:, :half]], axis=1)
    return turn * cos2 + swapped * sin2


def dot(a, b):
    return jnp.dot(a, b, preferred_element_type=F32)


def dot_nt(a, b):
    return lax.dot_general(a, b, (((1,), (1,)), ((), ())), preferred_element_type=F32)


def low_rank(x_rows, cos2, sin2, attn_g, kv_g, q_g, dkv, qa, out):
    q_rank = qa.shape[1]
    latent = kv_g.shape[1]
    width = dkv.shape[0]
    rows = x_rows.shape[0]
    normed = rms_norm(x_rows, attn_g)
    out[:, 0:q_rank] = rms_norm(dot(normed, qa[...]), q_g)
    kv_lat = dot_nt(normed, dkv[...])
    out[:, q_rank:q_rank + latent] = rms_norm(kv_lat[:, :latent], kv_g)
    turned = rotate(kv_lat[:, latent:], cos2, sin2).astype(BF16)
    pad = jnp.zeros((rows, out.shape[1] - q_rank - width), BF16)
    out[:, q_rank + latent:] = jnp.concatenate([turned, pad], axis=1)


def attention_kernel(layer, heads, nope, latent, lengths, given, cos_ref, sin_ref, attn_g, kv_g, q_g, cache, w_dkv, w_qa, w_qb, w_uk, w_uv, w_o, part, new_cache,
                     blocks, low, dkv, qa, qb, uk, uv, wo, entry, q_lat, q_rot, o_lat, o_cat, wsem, rsem, ssem):
    rows = cos_ref.shape[0]
    pitch = rows + PITCH_PAD
    slots = cache.shape[2]
    width = cache.shape[1]
    rope = width - latent
    qk = nope + rope
    q_rank = qb.shape[0]
    steps = rows // ROWS_PER_STEP
    weights = [(w_dkv, dkv), (w_qa, qa), (w_qb, qb), (w_uk, uk), (w_uv, uv), (w_o, wo)]

    def load_weight(n):
        return pltpu.make_async_copy(weights[n][0].at[layer], weights[n][1], wsem.at[n])

    def row_slice(step):
        return pl.ds(pl.multiple_of(step * ROWS_PER_STEP, ROWS_PER_STEP), ROWS_PER_STEP)

    def load(step, slot):
        return pltpu.make_async_copy(cache.at[row_slice(step)], blocks.at[slot], rsem.at[slot])

    def store(step, slot):
        return pltpu.make_async_copy(blocks.at[slot], new_cache.at[row_slice(step)], ssem.at[slot])

    first = layer == 0
    for n in ((0, 1) if first else ()) + (2, 3):
        load_weight(n).start()
    for step in range(AHEAD):
        load(step, step).start()
    load_weight(4).start()
    load_weight(5).start()

    cos2 = cos_ref[...]
    sin2 = sin_ref[...]
    if first:
        load_weight(0).wait()
        load_weight(1).wait()
        low_rank(given[...], cos2, sin2, attn_g[layer:layer + 1], kv_g[layer:layer + 1], q_g[layer:layer + 1], dkv, qa, low)
    else:
        low = given
    entry[...] = low[:, q_rank:].astype(F32)
    load_weight(2).wait()
    load_weight(3).wait()
    group = 4
    for g in range(heads // group):
        q_part = dot(low[:, :q_rank], qb[:, g * group * qk:(g + 1) * group * qk])
        for j in range(group):
            h = g * group + j
            mine = q_part[:, j * qk:(j + 1) * qk]
            q_rot[h * pitch:h * pitch + rows, 0:rope] = rotate(mine[:, nope:], cos2, sin2)
            latent_q = dot(mine[:, :nope].astype(BF16), uk[h])
            for c in range(latent // LANES):
                q_lat[c, h * pitch:h * pitch + rows, :] = latent_q[:, c * LANES:(c + 1) * LANES]

    scale = qk ** -0.5
    lane = lax.broadcasted_iota(jnp.int32, (1, slots), 1)

    def one_step(step, carry):
        slot = lax.rem(step, SLOTS)
        load(step, slot).wait()
        columns = jnp.transpose(entry[row_slice(step), :])
        probs = []
        for r in range(ROWS_PER_STEP):
            row = step * ROWS_PER_STEP + r
            length = lengths[row]
            fresh = jnp.broadcast_to(columns[:width, r:r + 1], (width, slots)).astype(BF16)
            blocks[slot, r] = jnp.where(lane == length, fresh, blocks[slot, r])
            lat = jnp.concatenate([q_lat.at[c][pl.ds(row, heads, stride=pitch), :] for c in range(latent // LANES)], axis=1).astype(BF16)
            rot = q_rot[pl.ds(row, heads, stride=pitch), :][:, :rope].astype(BF16)
            score = dot(lat, blocks[slot, r, :latent]) + dot(rot, blocks[slot, r, latent:])
            score = jnp.where(lane <= length, score * scale, -1e30)
            score = jnp.exp(score - jnp.max(score, axis=1, keepdims=True))
            probs.append((score * (1.0 / jnp.sum(score, axis=1, keepdims=True))).astype(BF16))
        for r in range(ROWS_PER_STEP):
            row = step * ROWS_PER_STEP + r
            mixed = dot_nt(probs[r], blocks[slot, r, :latent])
            for c in range(latent // LANES):
                o_lat.at[c][pl.ds(row, heads, stride=pitch), :] = mixed[:, c * LANES:(c + 1) * LANES]
        store(step, slot).start()

        @pl.when(step + AHEAD < steps)
        def _():
            @pl.when(step + AHEAD >= SLOTS)
            def _():
                store(step + AHEAD - SLOTS, lax.rem(step + AHEAD, SLOTS)).wait()
            load(step + AHEAD, lax.rem(step + AHEAD, SLOTS)).start()
        return carry

    lax.fori_loop(0, steps, one_step, 0)
    load_weight(4).wait()
    load_weight(5).wait()
    for h in range(0, heads, 2):
        pair = []
        for n in (h, h + 1):
            mixed = jnp.concatenate([o_lat[c, n * pitch:n * pitch + rows, :] for c in range(latent // LANES)], axis=1)
            pair.append(dot_nt(mixed.astype(BF16), uv[n]).astype(BF16))
        v = uv.shape[1]
        o_cat[:, h * v:(h + 2) * v] = jnp.concatenate(pair, axis=1)
    chunk = 512
    for n in range(wo.shape[1] // chunk):
        part[:, n * chunk:(n + 1) * chunk] = dot(o_cat[...], wo[:, n * chunk:(n + 1) * chunk])
    for step in range(max(steps - SLOTS, 0), steps):
        store(step, step % SLOTS).wait()


ANY = pl.BlockSpec(memory_space=pl.ANY)
VMEM = pl.BlockSpec(memory_space=pltpu.VMEM)
SMEM = pl.BlockSpec(memory_space=pltpu.SMEM)


def low_width(w_qa, w_dkv_t):
    return -(-(w_qa.shape[2] + w_dkv_t.shape[1]) // LANES) * LANES


def attention(layer, given, lengths, cache_t, cos2, sin2, gains, w_dkv_t, w_qa, w_qb, w_uk, w_uv_t, w_o):
    rows = lengths.shape[0]
    _, heads, nope, latent = w_uk.shape
    width, slots = cache_t.shape[1:]
    model = w_o.shape[2]
    padded = low_width(w_qa, w_dkv_t)
    q_rank = w_qa.shape[2]
    low_shapes = [((rows, padded), BF16), (w_dkv_t.shape[1:], BF16), (w_qa.shape[1:], BF16)]
    if layer:
        low_shapes = [((8, LANES), BF16)] * 3
    return pl.pallas_call(
        functools.partial(attention_kernel, layer, heads, nope, latent),
        out_shape=(jax.ShapeDtypeStruct((rows, model), F32), jax.ShapeDtypeStruct(cache_t.shape, BF16)),
        in_specs=[SMEM] + [VMEM] * 6 + [ANY] * 7,
        out_specs=(VMEM, ANY),
        scratch_shapes=[pltpu.VMEM((SLOTS, ROWS_PER_STEP, width, slots), BF16)] + [pltpu.VMEM(*s) for s in low_shapes] + [
            pltpu.VMEM(w_qb.shape[1:], BF16),
            pltpu.VMEM(w_uk.shape[1:], BF16),
            pltpu.VMEM(w_uv_t.shape[1:], BF16),
            pltpu.VMEM(w_o.shape[1:], BF16),
            pltpu.VMEM((rows, padded - q_rank), F32),
            pltpu.VMEM((latent // LANES, heads * (rows + PITCH_PAD), LANES), F32),
            pltpu.VMEM((heads * (rows + PITCH_PAD), LANES), F32),
            pltpu.VMEM((latent // LANES, heads * (rows + PITCH_PAD), LANES), F32),
            pltpu.VMEM((rows, w_o.shape[1]), BF16),
            pltpu.SemaphoreType.DMA((6,)),
            pltpu.SemaphoreType.DMA((SLOTS,)),
            pltpu.SemaphoreType.DMA((SLOTS,)),
        ],
        compiler_params=pltpu.CompilerParams(vmem_limit_bytes=VMEM_LIMIT),
        name="attention",
    )(lengths, given, cos2, sin2, *gains, cache_t, w_dkv_t, w_qa, w_qb, w_uk, w_uv_t, w_o)


def ffn_kernel(layer, last, part, x_in, cos_ref, sin_ref, ffn_g, attn_g, kv_g, q_g, w_gate, w_up, w_down, w_dkv, w_qa, *rest):
    if last:
        out, *rest = rest
        gates, ups, downs, arrived, x_mid, g_pair, hidden, mine, outgoing, incoming, x_new, x_far, sems, dsem, ssem, rsem = rest
    else:
        low_out, x_out, *rest = rest
        gates, ups, downs, arrived, x_mid, g_pair, hidden, mine, outgoing, incoming, low_mine, low_far, dkv, qa, sems, dsem, lsem, ssem, rsem = rest
    tp = lax.axis_index("tp")
    dp = lax.axis_index("dp")
    core = lax.rem(dp, 2)
    peer = {"tp": 1 - tp}
    mate = {"dp": dp + 1 - 2 * core}
    half, model = arrived.shape
    h_block = gates.shape[2]
    h_width = hidden.shape[1]
    o_block = downs.shape[2]
    own = pl.ds(pl.multiple_of(tp * half, half), half)
    far = pl.ds(pl.multiple_of((1 - tp) * half, half), half)

    def hidden_loads(b, slot):
        cols = pl.ds(pl.multiple_of(core * h_width + b * h_block, LANES), h_block)
        return [pltpu.make_async_copy(w.at[layer, :, cols], v.at[slot], sems.at[n, slot]) for n, (w, v) in enumerate(((w_gate, gates), (w_up, ups)))]

    def down_load(c):
        return pltpu.make_async_copy(w_down.at[layer, pl.ds(pl.multiple_of(core * h_width, LANES), h_width), pl.ds(c * o_block, o_block)], downs.at[c], dsem.at[c])

    for b in range(HIDDEN_SLOTS):
        for copy in hidden_loads(b, b):
            copy.start()
    for c in range(OUT_BLOCKS):
        down_load(c).start()
    if not last:
        loads = [pltpu.make_async_copy(w_dkv.at[layer + 1], dkv, lsem.at[0]), pltpu.make_async_copy(w_qa.at[layer + 1], qa, lsem.at[1])]
        for copy in loads:
            copy.start()

    barrier = pltpu.get_barrier_semaphore()
    for other in (peer, mate):
        pl.semaphore_signal(barrier, inc=1, device_id=other, device_id_type=MESH)
    pl.semaphore_wait(barrier, 2)

    def send(src, dst, n, to):
        return pltpu.make_async_remote_copy(src_ref=src, dst_ref=dst, send_sem=ssem.at[n], recv_sem=rsem.at[n], device_id=to, device_id_type=MESH)

    scatter = send(part.at[far], arrived, 0, peer)
    scatter.start()
    x_own = x_in[own, :] if layer == 0 else x_in[...]
    scatter.wait_recv()
    x_mid[...] = (x_own.astype(F32) + (part[own, :] + arrived[...])).astype(BF16)
    g_pair[0:half, :] = rms_norm(x_mid[...], ffn_g[layer:layer + 1])
    swap = send(g_pair.at[0:half], g_pair.at[half:2 * half], 1, mate)
    swap.start()
    swap.wait_recv()

    def hidden_step(b, carry):
        slot = lax.rem(b, HIDDEN_SLOTS)
        for copy in hidden_loads(b, slot):
            copy.wait()
        gate = dot(g_pair[...], gates[slot])
        up = dot(g_pair[...], ups[slot])
        hidden[:, pl.ds(pl.multiple_of(b * h_block, LANES), h_block)] = (jax.nn.silu(gate) * up).astype(BF16)

        @pl.when(b + HIDDEN_SLOTS < HIDDEN_BLOCKS)
        def _():
            for copy in hidden_loads(b + HIDDEN_SLOTS, slot):
                copy.start()
        return carry

    lax.fori_loop(0, HIDDEN_BLOCKS, hidden_step, 0)

    returns = [send(outgoing.at[c], incoming.at[c], 2 + c, mate) for c in range(OUT_BLOCKS)]
    if last:
        spreads = [send(x_new.at[c], x_far.at[c], 2 + OUT_BLOCKS + c, peer) for c in range(OUT_BLOCKS)]

    def finish(c):
        returns[c].wait_recv()
        cols = slice(c * o_block, (c + 1) * o_block)
        fresh = (x_mid[:, cols].astype(F32) + (mine[:, cols] + incoming[c].astype(F32))).astype(BF16)
        if last:
            x_new[c] = fresh
            spreads[c].start()
            out[own, cols] = fresh
        else:
            x_out[:, cols] = fresh

    for c in range(OUT_BLOCKS):
        down_load(c).wait()
        y = dot(hidden[...], downs[c])
        outgoing[c] = y[half:].astype(BF16)
        returns[c].start()
        mine[:, c * o_block:(c + 1) * o_block] = y[:half]
        if c:
            finish(c - 1)
    finish(OUT_BLOCKS - 1)

    if last:
        for c in range(OUT_BLOCKS):
            spreads[c].wait_recv()
            out[far, c * o_block:(c + 1) * o_block] = x_far[c]
            spreads[c].wait_send()
    else:
        for copy in loads:
            copy.wait()
        nxt = layer + 1
        low_rank(x_out[...], cos_ref[own, :], sin_ref[own, :], attn_g[nxt:nxt + 1], kv_g[nxt:nxt + 1], q_g[nxt:nxt + 1], dkv, qa, low_mine)
        share = send(low_mine, low_far, 2 + OUT_BLOCKS, peer)
        share.start()
        low_out[own, :] = low_mine[...]
        share.wait_recv()
        low_out[far, :] = low_far[...]
        share.wait_send()
    scatter.wait_send()
    swap.wait_send()
    for c in range(OUT_BLOCKS):
        returns[c].wait_send()


def ffn(layer, last, part, x_in, cos2, sin2, ffn_gain, gains, w_gate, w_up, w_down, w_dkv_t, w_qa):
    rows, model = part.shape
    half = rows // 2
    h_width = w_gate.shape[2] // 2
    h_block = h_width // HIDDEN_BLOCKS
    o_block = model // OUT_BLOCKS
    padded = low_width(w_qa, w_dkv_t)
    scratch = [
        pltpu.VMEM((HIDDEN_SLOTS, model, h_block), BF16),
        pltpu.VMEM((HIDDEN_SLOTS, model, h_block), BF16),
        pltpu.VMEM((OUT_BLOCKS, h_width, o_block), BF16),
        pltpu.VMEM((half, model), F32),
        pltpu.VMEM((half, model), BF16),
        pltpu.VMEM((rows, model), BF16),
        pltpu.VMEM((rows, h_width), BF16),
        pltpu.VMEM((half, model), F32),
        pltpu.VMEM((OUT_BLOCKS, half, o_block), BF16),
        pltpu.VMEM((OUT_BLOCKS, half, o_block), BF16),
    ]
    dma = pltpu.SemaphoreType.DMA
    if last:
        out_shape = jax.ShapeDtypeStruct((rows, model), BF16)
        out_specs = VMEM
        scratch += [pltpu.VMEM((OUT_BLOCKS, half, o_block), BF16)] * 2 + [dma((2, HIDDEN_SLOTS)), dma((OUT_BLOCKS,))]
    else:
        out_shape = (jax.ShapeDtypeStruct((rows, padded), BF16), jax.ShapeDtypeStruct((half, model), BF16))
        out_specs = (VMEM, VMEM)
        scratch += [pltpu.VMEM((half, padded), BF16)] * 2 + [pltpu.VMEM(w_dkv_t.shape[1:], BF16), pltpu.VMEM(w_qa.shape[1:], BF16)]
        scratch += [dma((2, HIDDEN_SLOTS)), dma((OUT_BLOCKS,)), dma((2,))]
    copies = 2 + OUT_BLOCKS + (OUT_BLOCKS if last else 1)
    return pl.pallas_call(
        functools.partial(ffn_kernel, layer, last),
        out_shape=out_shape,
        in_specs=[VMEM] * 8 + [ANY] * 5,
        out_specs=out_specs,
        scratch_shapes=scratch + [dma((copies,)), dma((copies,))],
        compiler_params=pltpu.CompilerParams(vmem_limit_bytes=VMEM_LIMIT, collective_id=layer, has_side_effects=True),
        name="ffn",
    )(part, x_in, cos2, sin2, ffn_gain, *gains, w_gate, w_up, w_down, w_dkv_t, w_qa)


def solution(mesh):
    row_spec = P(('rep', 'dp'), None)
    cache_spec = P(('rep', 'dp'), None, None)
    in_specs = (row_spec, P(('rep', 'dp')), cache_spec, cache_spec, P(), P(), P(), P(), P(), P(), P(None, None, 'tp'), P(None, 'tp', None, None), P(None, 'tp', None, None), P(None, 'tp', None), P(), P(), P())
    out_specs = (row_spec, cache_spec, cache_spec)

    def local_step(x, lengths, cache0, cache1, attn_gain, kv_gain, q_gain, ffn_gain, w_dkv, w_qa, w_qb, w_uk, w_uv, w_o, w_gate, w_up, w_down):
        cos2, sin2 = rope_tables(lengths, cache0.shape[2] - w_uk.shape[3])
        w_uv_t = jnp.swapaxes(w_uv, 2, 3)
        w_dkv_t = jnp.swapaxes(w_dkv, 1, 2)
        gains = (attn_gain, kv_gain, q_gain)
        caches = (cache0, cache1)
        given = x
        new_caches = []
        for i, cache in enumerate(caches):
            part, new_cache = attention(i, given, lengths, jnp.swapaxes(cache, 1, 2), cos2, sin2, gains, w_dkv_t, w_qa, w_qb, w_uk, w_uv_t, w_o)
            new_caches.append(jnp.swapaxes(new_cache, 1, 2))
            last = i == len(caches) - 1
            result = ffn(i, last, part, x, cos2, sin2, ffn_gain, gains, w_gate, w_up, w_down, w_dkv_t, w_qa)
            if not last:
                given, x = result
        return result, new_caches[0], new_caches[1]

    return jax.shard_map(local_step, mesh=mesh, in_specs=in_specs, out_specs=out_specs, check_vma=False)
```

profile of v0, /device:TPU:0, one launch (start us, length us, event | category | flops | bytes accessed | tf_op | source)
XLA Modules:
  0.0 138.1 jit_solution(3177933541451684670)
XLA Ops:
  0.6 0.7 convert_element_type.10
  1.3 0.1 fusion
  1.4 0.7 copy.20.cos_ref
  2.2 0.7 copy.21.sin_ref
  2.9 28.0 %attention.2 = (f32[128,2560]{1,0:T(8,128)}, bf16[128,288,256]{2,1,0:T(8,128)(2,1)}) custom-call(s32[128]{0:T(128)} %lengths.3, bf16[128,2560]{1,0:T(8,128)(2,1)} %x_in.1, f32[128,32]{1,0:T(8,128)} %copy.20.cos_ref, f32[128,32]{1,0:T(8,128)} %copy.21.sin_ref, f32[2,2560]{1,0:T(2,128)} %attn_g.7, f32[2,256]{1,0:T(2,128)} %kv_g.7, f32[2,768]{1,0:T(2,128)} %q_g.7, ...), custom_call_target="tpu_custom_call" | custom-call | tf_op jit(solution)/shard_map/attention/pallas_call | solution.py:192
  30.9 41.2 %ffn.2 = (bf16[128,1152]{1,0:T(8,128)(2,1)}, bf16[64,2560]{1,0:T(8,128)(2,1)}) custom-call(f32[128,2560]{1,0:T(8,128)} %get-tuple-element.9.part, bf16[128,2560]{1,0:T(8,128)(2,1)} %x_in.1, f32[128,32]{1,0:T(8,128)} %copy.20.cos_ref, f32[128,32]{1,0:T(8,128)} %copy.21.sin_ref, f32[2,2560]{1,0:T(2,128)} %ffn_g.3, f32[2,2560]{1,0:T(2,128)} %attn_g.7, ...), custom_call_target="tpu_custom_call" | custom-call | tf_op jit(solution)/shard_map/ffn/pallas_call | solution.py:363
  72.1 26.1 %attention.3 = (f32[128,2560]{1,0:T(8,128)}, bf16[128,288,256]{2,1,0:T(8,128)(2,1)}) custom-call(s32[128]{0:T(128)} %lengths.3, bf16[128,1152]{1,0:T(8,128)(2,1)} %get-tuple-element.10.given, f32[128,32]{1,0:T(8,128)} %copy.20.cos_ref, f32[128,32]{1,0:T(8,128)} %copy.21.sin_ref, f32[2,2560]{1,0:T(2,128)} %attn_g.7, f32[2,256]{1,0:T(2,128)} %kv_g.7, ...), custom_call_target="tpu_custom_call" | custom-call | tf_op jit(solution)/shard_map/attention/pallas_call | solution.py:192
  98.2 37.9 %ffn.3 = bf16[128,2560]{1,0:T(8,128)(2,1)} custom-call(f32[128,2560]{1,0:T(8,128)} %get-tuple-element.11.part, bf16[64,2560]{1,0:T(8,128)(2,1)} %get-tuple-element.12.x_in, f32[128,32]{1,0:T(8,128)} %copy.20.cos_ref, f32[128,32]{1,0:T(8,128)} %copy.21.sin_ref, f32[2,2560]{1,0:T(2,128)} %ffn_g.3, f32[2,2560]{1,0:T(2,128)} %attn_g.7, f32[2,256]{1,0:T(2,128)} %kv_g.7, ...), custom_call_target="tpu_custom_call" | custom-call | tf_op jit(solution)/shard_map/ffn/pallas_call | solution.py:363
  136.1 2.0 %copy.29 = bf16[128,2560]{1,0:T(8,128)(2,1)} copy(bf16[128,2560]{1,0:T(8,128)(2,1)} %ffn.3) | data formatting | bytes 1310720
  (2 shorter events, 0.0 us)
where the time goes:
time: 138 us
  Pallas kernels  133 us (96%)
  local copies, waits for them, and re-layouts  3.41 us (2%)
    pallas_call x2, Pallas kernels, ffn(): pl.pallas_call(functools.partial(ffn_kernel, layer, last), out_shape=out_...  79.1 us
    pallas_call x2, Pallas kernels, attention(): pl.pallas_call(functools.partial(attention_kernel, layer, heads, nope, la...  54.1 us

commit v1 on v0

--- a/solution.py
+++ b/solution.py
@@ -11,9 +11,9 @@
 ROPE_BASE = 10000.0
 F32 = jnp.float32
 BF16 = jnp.bfloat16
-ROWS_PER_STEP = 8
-SLOTS = 12
-AHEAD = 8
+ROWS_PER_STEP = 16
+SLOTS = 5
+OUT_SLOTS = 3
 LANES = 128
 PITCH_PAD = 8
 HIDDEN_BLOCKS = 5
@@ -31,16 +31,17 @@
 
 def rope_tables(lengths, rope_dim):
     half_dim = rope_dim // 2
-    inv_freq = ROPE_BASE ** (-2.0 * jnp.arange(half_dim).astype(F32) / rope_dim)
+    lane = jnp.arange(LANES)
+    inv_freq = ROPE_BASE ** (-2.0 * (lane % half_dim).astype(F32) / rope_dim)
     angles = lengths.astype(F32)[:, None] * inv_freq[None, :]
-    cos_tab, sin_tab = jnp.cos(angles), jnp.sin(angles)
-    return jnp.concatenate([cos_tab, cos_tab], axis=1), jnp.concatenate([-sin_tab, sin_tab], axis=1)
-
-
-def rotate(turn, cos2, sin2):
+    sines = jnp.sin(angles)
+    return jnp.where(lane < rope_dim, jnp.cos(angles), jnp.where(lane % rope_dim < half_dim, -sines, sines))
+
+
+def rotate(turn, table):
     half = turn.shape[1] // 2
     swapped = jnp.concatenate([turn[:, half:], turn[:, :half]], axis=1)
-    return turn * cos2 + swapped * sin2
+    return turn * table[:, :2 * half] + swapped * table[:, 2 * half:4 * half]
 
 
 def dot(a, b):
@@ -51,7 +52,7 @@
     return lax.dot_general(a, b, (((1,), (1,)), ((), ())), preferred_element_type=F32)
 
 
-def low_rank(x_rows, cos2, sin2, attn_g, kv_g, q_g, dkv, qa, out):
+def low_rank(x_rows, table, attn_g, kv_g, q_g, dkv, qa, out):
     q_rank = qa.shape[1]
     latent = kv_g.shape[1]
     width = dkv.shape[0]
@@ -60,14 +61,14 @@
     out[:, 0:q_rank] = rms_norm(dot(normed, qa[...]), q_g)
     kv_lat = dot_nt(normed, dkv[...])
     out[:, q_rank:q_rank + latent] = rms_norm(kv_lat[:, :latent], kv_g)
-    turned = rotate(kv_lat[:, latent:], cos2, sin2).astype(BF16)
+    turned = rotate(kv_lat[:, latent:], table).astype(BF16)
     pad = jnp.zeros((rows, out.shape[1] - q_rank - width), BF16)
     out[:, q_rank + latent:] = jnp.concatenate([turned, pad], axis=1)
 
 
-def attention_kernel(layer, heads, nope, latent, lengths, given, cos_ref, sin_ref, attn_g, kv_g, q_g, cache, w_dkv, w_qa, w_qb, w_uk, w_uv, w_o, part, new_cache,
-                     blocks, low, dkv, qa, qb, uk, uv, wo, entry, q_lat, q_rot, o_lat, o_cat, wsem, rsem, ssem):
-    rows = cos_ref.shape[0]
+def attention_kernel(layer, heads, nope, latent, lengths, given, table_ref, attn_g, kv_g, q_g, cache, w_dkv, w_qa, w_qb, w_uk, w_uv, w_o, part, new_cache,
+                     blocks, outs, low, dkv, qa, qb, uk, uv, wo, entry, q_lat, q_rot, o_lat, o_cat, wsem, rsem, ssem):
+    rows = table_ref.shape[0]
     pitch = rows + PITCH_PAD
     slots = cache.shape[2]
     width = cache.shape[1]
@@ -87,22 +88,21 @@
         return pltpu.make_async_copy(cache.at[row_slice(step)], blocks.at[slot], rsem.at[slot])
 
     def store(step, slot):
-        return pltpu.make_async_copy(blocks.at[slot], new_cache.at[row_slice(step)], ssem.at[slot])
+        return pltpu.make_async_copy(outs.at[slot], new_cache.at[row_slice(step)], ssem.at[slot])
 
     first = layer == 0
     for n in ((0, 1) if first else ()) + (2, 3):
         load_weight(n).start()
-    for step in range(AHEAD):
+    for step in range(SLOTS):
         load(step, step).start()
     load_weight(4).start()
     load_weight(5).start()
 
-    cos2 = cos_ref[...]
-    sin2 = sin_ref[...]
+    table = table_ref[...]
     if first:
         load_weight(0).wait()
         load_weight(1).wait()
-        low_rank(given[...], cos2, sin2, attn_g[layer:layer + 1], kv_g[layer:layer + 1], q_g[layer:layer + 1], dkv, qa, low)
+        low_rank(given[...], table, attn_g[layer:layer + 1], kv_g[layer:layer + 1], q_g[layer:layer + 1], dkv, qa, low)
     else:
         low = given
     entry[...] = low[:, q_rank:].astype(F32)
@@ -114,10 +114,10 @@
         for j in range(group):
             h = g * group + j
             mine = q_part[:, j * qk:(j + 1) * qk]
-            q_rot[h * pitch:h * pitch + rows, 0:rope] = rotate(mine[:, nope:], cos2, sin2)
+            q_rot[h * pitch:h * pitch + rows, :] = jnp.concatenate([rotate(mine[:, nope:], table).astype(BF16).astype(F32), jnp.zeros((rows, LANES - rope), F32)], axis=1)
             latent_q = dot(mine[:, :nope].astype(BF16), uk[h])
             for c in range(latent // LANES):
-                q_lat[c, h * pitch:h * pitch + rows, :] = latent_q[:, c * LANES:(c + 1) * LANES]
+                q_lat[c, h * pitch:h * pitch + rows, :] = latent_q[:, c * LANES:(c + 1) * LANES].astype(BF16).astype(F32)
 
     scale = qk ** -0.5
     lane = lax.broadcasted_iota(jnp.int32, (1, slots), 1)
@@ -125,32 +125,48 @@
     def one_step(step, carry):
         slot = lax.rem(step, SLOTS)
         load(step, slot).wait()
-        columns = jnp.transpose(entry[row_slice(step), :])
-        probs = []
+        drain = lax.rem(step, OUT_SLOTS)
+
+        @pl.when(step >= OUT_SLOTS)
+        def _():
+            store(step - OUT_SLOTS, drain).wait()
+
+        fresh_rows = entry[row_slice(step), :]
+        columns = jnp.transpose(fresh_rows)
+        scores, probs, news = [], [], []
         for r in range(ROWS_PER_STEP):
             row = step * ROWS_PER_STEP + r
-            length = lengths[row]
-            fresh = jnp.broadcast_to(columns[:width, r:r + 1], (width, slots)).astype(BF16)
-            blocks[slot, r] = jnp.where(lane == length, fresh, blocks[slot, r])
-            lat = jnp.concatenate([q_lat.at[c][pl.ds(row, heads, stride=pitch), :] for c in range(latent // LANES)], axis=1).astype(BF16)
-            rot = q_rot[pl.ds(row, heads, stride=pitch), :][:, :rope].astype(BF16)
-            score = dot(lat, blocks[slot, r, :latent]) + dot(rot, blocks[slot, r, latent:])
-            score = jnp.where(lane <= length, score * scale, -1e30)
-            score = jnp.exp(score - jnp.max(score, axis=1, keepdims=True))
-            probs.append((score * (1.0 / jnp.sum(score, axis=1, keepdims=True))).astype(BF16))
+            lat = jnp.concatenate([q_lat.at[c][pl.ds(row, heads, stride=pitch), :] for c in range(latent // LANES)], axis=1)
+            rot = q_rot[pl.ds(row, heads, stride=pitch), :]
+            new_score = lat * fresh_rows[r:r + 1, :latent]
+            new_score = jnp.sum(new_score[:, :LANES] + new_score[:, LANES:] + rot * fresh_rows[r:r + 1, latent:], axis=1, keepdims=True)
+            score = dot(lat.astype(BF16), blocks[slot, r, :latent]) + dot(rot[:, :rope].astype(BF16), blocks[slot, r, latent:])
+            scores.append(score)
+            news.append(new_score)
+        for r in range(ROWS_PER_STEP):
+            length = lengths[step * ROWS_PER_STEP + r]
+            new_score = news[r] * scale
+            score = jnp.where(lane < length, scores[r] * scale, -1e30)
+            top = jnp.maximum(jnp.max(score, axis=1, keepdims=True), new_score)
+            score = jnp.exp(score - top)
+            new_score = jnp.exp(new_score - top)
+            inverse = 1.0 / (jnp.sum(score, axis=1, keepdims=True) + new_score)
+            probs.append((score * inverse).astype(BF16))
+            news[r] = (new_score * inverse).astype(BF16).astype(F32)
         for r in range(ROWS_PER_STEP):
             row = step * ROWS_PER_STEP + r
-            mixed = dot_nt(probs[r], blocks[slot, r, :latent])
+            mixed = dot_nt(probs[r], blocks[slot, r, :latent]) + news[r] * fresh_rows[r:r + 1, :latent]
             for c in range(latent // LANES):
                 o_lat.at[c][pl.ds(row, heads, stride=pitch), :] = mixed[:, c * LANES:(c + 1) * LANES]
-        store(step, slot).start()
-
-        @pl.when(step + AHEAD < steps)
+        for r in range(ROWS_PER_STEP):
+            length = lengths[step * ROWS_PER_STEP + r]
+            fresh = jnp.broadcast_to(columns[:width, r:r + 1], (width, slots)).astype(BF16)
+            outs[drain, r] = jnp.where(lane == length, fresh, blocks[slot, r])
+        store(step, drain).start()
+
+        @pl.when(step + SLOTS < steps)
         def _():
-            @pl.when(step + AHEAD >= SLOTS)
-            def _():
-                store(step + AHEAD - SLOTS, lax.rem(step + AHEAD, SLOTS)).wait()
-            load(step + AHEAD, lax.rem(step + AHEAD, SLOTS)).start()
+            load(step + SLOTS, slot).start()
         return carry
 
     lax.fori_loop(0, steps, one_step, 0)
@@ -166,8 +182,8 @@
     chunk = 512
     for n in range(wo.shape[1] // chunk):
         part[:, n * chunk:(n + 1) * chunk] = dot(o_cat[...], wo[:, n * chunk:(n + 1) * chunk])
-    for step in range(max(steps - SLOTS, 0), steps):
-        store(step, step % SLOTS).wait()
+    for step in range(max(steps - OUT_SLOTS, 0), steps):
+        store(step, step % OUT_SLOTS).wait()
 
 
 ANY = pl.BlockSpec(memory_space=pl.ANY)
@@ -179,7 +195,7 @@
     return -(-(w_qa.shape[2] + w_dkv_t.shape[1]) // LANES) * LANES
 
 
-def attention(layer, given, lengths, cache_t, cos2, sin2, gains, w_dkv_t, w_qa, w_qb, w_uk, w_uv_t, w_o):
+def attention(layer, given, lengths, cache_t, table, gains, w_dkv_t, w_qa, w_qb, w_uk, w_uv_t, w_o):
     rows = lengths.shape[0]
     _, heads, nope, latent = w_uk.shape
     width, slots = cache_t.shape[1:]
@@ -192,9 +208,9 @@
     return pl.pallas_call(
         functools.partial(attention_kernel, layer, heads, nope, latent),
         out_shape=(jax.ShapeDtypeStruct((rows, model), F32), jax.ShapeDtypeStruct(cache_t.shape, BF16)),
-        in_specs=[SMEM] + [VMEM] * 6 + [ANY] * 7,
+        in_specs=[SMEM] + [VMEM] * 5 + [ANY] * 7,
         out_specs=(VMEM, ANY),
-        scratch_shapes=[pltpu.VMEM((SLOTS, ROWS_PER_STEP, width, slots), BF16)] + [pltpu.VMEM(*s) for s in low_shapes] + [
+        scratch_shapes=[pltpu.VMEM((n, ROWS_PER_STEP, width, slots), BF16) for n in (SLOTS, OUT_SLOTS)] + [pltpu.VMEM(*s) for s in low_shapes] + [
             pltpu.VMEM(w_qb.shape[1:], BF16),
             pltpu.VMEM(w_uk.shape[1:], BF16),
             pltpu.VMEM(w_uv_t.shape[1:], BF16),
@@ -206,27 +222,27 @@
             pltpu.VMEM((rows, w_o.shape[1]), BF16),
             pltpu.SemaphoreType.DMA((6,)),
             pltpu.SemaphoreType.DMA((SLOTS,)),
-            pltpu.SemaphoreType.DMA((SLOTS,)),
+            pltpu.SemaphoreType.DMA((OUT_SLOTS,)),
         ],
         compiler_params=pltpu.CompilerParams(vmem_limit_bytes=VMEM_LIMIT),
         name="attention",
-    )(lengths, given, cos2, sin2, *gains, cache_t, w_dkv_t, w_qa, w_qb, w_uk, w_uv_t, w_o)
-
-
-def ffn_kernel(layer, last, part, x_in, cos_ref, sin_ref, ffn_g, attn_g, kv_g, q_g, w_gate, w_up, w_down, w_dkv, w_qa, *rest):
+    )(lengths, given, table, *gains, cache_t, w_dkv_t, w_qa, w_qb, w_uk, w_uv_t, w_o)
+
+
+def ffn_kernel(layer, last, part, x_in, table_ref, ffn_g, attn_g, kv_g, q_g, w_gate, w_up, w_down, w_dkv, w_qa, *rest):
     if last:
-        out, *rest = rest
-        gates, ups, downs, arrived, x_mid, g_pair, hidden, mine, outgoing, incoming, x_new, x_far, sems, dsem, ssem, rsem = rest
+        out_own, out_far, *rest = rest
+        wides, downs, arrived, x_mid, g_pair, hidden, mine, outgoing, incoming, x_new, x_far, sems, dsem, ssem, rsem = rest
     else:
         low_out, x_out, *rest = rest
-        gates, ups, downs, arrived, x_mid, g_pair, hidden, mine, outgoing, incoming, low_mine, low_far, dkv, qa, sems, dsem, lsem, ssem, rsem = rest
+        wides, downs, arrived, x_mid, g_pair, hidden, mine, outgoing, incoming, low_mine, low_far, dkv, qa, sems, dsem, lsem, ssem, rsem = rest
     tp = lax.axis_index("tp")
     dp = lax.axis_index("dp")
     core = lax.rem(dp, 2)
     peer = {"tp": 1 - tp}
     mate = {"dp": dp + 1 - 2 * core}
     half, model = arrived.shape
-    h_block = gates.shape[2]
+    h_block = wides.shape[2] // 2
     h_width = hidden.shape[1]
     o_block = downs.shape[2]
     own = pl.ds(pl.multiple_of(tp * half, half), half)
@@ -234,7 +250,7 @@
 
     def hidden_loads(b, slot):
         cols = pl.ds(pl.multiple_of(core * h_width + b * h_block, LANES), h_block)
-        return [pltpu.make_async_copy(w.at[layer, :, cols], v.at[slot], sems.at[n, slot]) for n, (w, v) in enumerate(((w_gate, gates), (w_up, ups)))]
+        return [pltpu.make_async_copy(w.at[layer, :, cols], wides.at[slot, :, pl.ds(n * h_block, h_block)], sems.at[n, slot]) for n, w in enumerate((w_gate, w_up))]
 
     def down_load(c):
         return pltpu.make_async_copy(w_down.at[layer, pl.ds(pl.multiple_of(core * h_width, LANES), h_width), pl.ds(c * o_block, o_block)], downs.at[c], dsem.at[c])
@@ -271,8 +287,8 @@
         slot = lax.rem(b, HIDDEN_SLOTS)
         for copy in hidden_loads(b, slot):
             copy.wait()
-        gate = dot(g_pair[...], gates[slot])
-        up = dot(g_pair[...], ups[slot])
+        both = dot(g_pair[...], wides[slot])
+        gate, up = both[:, :h_block], both[:, h_block:]
         hidden[:, pl.ds(pl.multiple_of(b * h_block, LANES), h_block)] = (jax.nn.silu(gate) * up).astype(BF16)
 
         @pl.when(b + HIDDEN_SLOTS < HIDDEN_BLOCKS)
@@ -294,7 +310,7 @@
         if last:
             x_new[c] = fresh
             spreads[c].start()
-            out[own, cols] = fresh
+            out_own[:, cols] = fresh
         else:
             x_out[:, cols] = fresh
 
@@ -311,13 +327,13 @@
     if last:
         for c in range(OUT_BLOCKS):
             spreads[c].wait_recv()
-            out[far, c * o_block:(c + 1) * o_block] = x_far[c]
+            out_far[:, c * o_block:(c + 1) * o_block] = x_far[c]
             spreads[c].wait_send()
     else:
         for copy in loads:
             copy.wait()
         nxt = layer + 1
-        low_rank(x_out[...], cos_ref[own, :], sin_ref[own, :], attn_g[nxt:nxt + 1], kv_g[nxt:nxt + 1], q_g[nxt:nxt + 1], dkv, qa, low_mine)
+        low_rank(x_out[...], table_ref[own, :], attn_g[nxt:nxt + 1], kv_g[nxt:nxt + 1], q_g[nxt:nxt + 1], dkv, qa, low_mine)
         share = send(low_mine, low_far, 2 + OUT_BLOCKS, peer)
         share.start()
         low_out[own, :] = low_mine[...]
@@ -330,7 +346,7 @@
         returns[c].wait_send()
 
 
-def ffn(layer, last, part, x_in, cos2, sin2, ffn_gain, gains, w_gate, w_up, w_down, w_dkv_t, w_qa):
+def ffn(layer, last, part, x_in, table, ffn_gain, gains, w_gate, w_up, w_down, w_dkv_t, w_qa):
     rows, model = part.shape
     half = rows // 2
     h_width = w_gate.shape[2] // 2
@@ -338,8 +354,7 @@
     o_block = model // OUT_BLOCKS
     padded = low_width(w_qa, w_dkv_t)
     scratch = [
-        pltpu.VMEM((HIDDEN_SLOTS, model, h_block), BF16),
-        pltpu.VMEM((HIDDEN_SLOTS, model, h_block), BF16),
+        pltpu.VMEM((HIDDEN_SLOTS, model, 2 * h_block), BF16),
         pltpu.VMEM((OUT_BLOCKS, h_width, o_block), BF16),
         pltpu.VMEM((half, model), F32),
         pltpu.VMEM((half, model), BF16),
@@ -351,8 +366,8 @@
     ]
     dma = pltpu.SemaphoreType.DMA
     if last:
-        out_shape = jax.ShapeDtypeStruct((rows, model), BF16)
-        out_specs = VMEM
+        out_shape = (jax.ShapeDtypeStruct((half, model), BF16),) * 2
+        out_specs = (VMEM, VMEM)
         scratch += [pltpu.VMEM((OUT_BLOCKS, half, o_block), BF16)] * 2 + [dma((2, HIDDEN_SLOTS)), dma((OUT_BLOCKS,))]
     else:
         out_shape = (jax.ShapeDtypeStruct((rows, padded), BF16), jax.ShapeDtypeStruct((half, model), BF16))
@@ -363,12 +378,12 @@
     return pl.pallas_call(
         functools.partial(ffn_kernel, layer, last),
         out_shape=out_shape,
-        in_specs=[VMEM] * 8 + [ANY] * 5,
+        in_specs=[VMEM] * 7 + [ANY] * 5,
         out_specs=out_specs,
         scratch_shapes=scratch + [dma((copies,)), dma((copies,))],
         compiler_params=pltpu.CompilerParams(vmem_limit_bytes=VMEM_LIMIT, collective_id=layer, has_side_effects=True),
         name="ffn",
-    )(part, x_in, cos2, sin2, ffn_gain, *gains, w_gate, w_up, w_down, w_dkv_t, w_qa)
+    )(part, x_in, table, ffn_gain, *gains, w_gate, w_up, w_down, w_dkv_t, w_qa)
 
 
 def solution(mesh):
@@ -378,7 +393,7 @@
     out_specs = (row_spec, cache_spec, cache_spec)
 
     def local_step(x, lengths, cache0, cache1, attn_gain, kv_gain, q_gain, ffn_gain, w_dkv, w_qa, w_qb, w_uk, w_uv, w_o, w_gate, w_up, w_down):
-        cos2, sin2 = rope_tables(lengths, cache0.shape[2] - w_uk.shape[3])
+        table = rope_tables(lengths, cache0.shape[2] - w_uk.shape[3])
         w_uv_t = jnp.swapaxes(w_uv, 2, 3)
         w_dkv_t = jnp.swapaxes(w_dkv, 1, 2)
         gains = (attn_gain, kv_gain, q_gain)
@@ -386,12 +401,14 @@
         given = x
         new_caches = []
         for i, cache in enumerate(caches):
-            part, new_cache = attention(i, given, lengths, jnp.swapaxes(cache, 1, 2), cos2, sin2, gains, w_dkv_t, w_qa, w_qb, w_uk, w_uv_t, w_o)
+            part, new_cache = attention(i, given, lengths, jnp.swapaxes(cache, 1, 2), table, gains, w_dkv_t, w_qa, w_qb, w_uk, w_uv_t, w_o)
             new_caches.append(jnp.swapaxes(new_cache, 1, 2))
             last = i == len(caches) - 1
-            result = ffn(i, last, part, x, cos2, sin2, ffn_gain, gains, w_gate, w_up, w_down, w_dkv_t, w_qa)
+            result = ffn(i, last, part, x, table, ffn_gain, gains, w_gate, w_up, w_down, w_dkv_t, w_qa)
             if not last:
                 given, x = result
-        return result, new_caches[0], new_caches[1]
+        mine, other = result
+        x_out = jnp.where(lax.axis_index('tp') == 0, jnp.concatenate([mine, other], 0), jnp.concatenate([other, mine], 0))
+        return x_out, new_caches[0], new_caches[1]
 
     return jax.shard_map(local_step, mesh=mesh, in_specs=in_specs, out_specs=out_specs, check_vma=False)

time: 138 us -> 124 us (0.90)
  Pallas kernels: 133 us -> 119 us
  local copies, waits for them, and re-layouts: 3.41 us -> 0 us
  other arithmetic: 0.79 us -> 3.91 us
    pallas_call x2, Pallas kernels: 54.1 us -> 39.3 us  [attention(): pl.pallas_call(functools.partial(attention_kernel, layer, heads, nope, la...]
    select_n x0 -> x2, other arithmetic: none -> 3.24 us  [the longest x1 2.28 us: local_step(): jnp.where(lax.axis_index('tp') == 0, jnp.concatenate([mine, other], 0), j...]
    unnamed x1 -> x0, local copies, waits for them, and re-layouts: 1.97 us -> none
    concatenate x2 -> x0, local copies, waits for them, and re-layouts: 1.44 us -> none  [the longest x1 0.73 us: rope_tables(): jnp.concatenate([cos_tab, cos_tab], axis=1)]
where the time goes in v1:
time: 124 us; the launch traced here: 123 us
  Pallas kernels  119 us (96%)
  other arithmetic  3.91 us (3%)
    pallas_call x2, Pallas kernels, ffn(): pl.pallas_call(functools.partial(ffn_kernel, layer, last), out_shape=out_...  79.5 us
    pallas_call x2, Pallas kernels, attention(): pl.pallas_call(functools.partial(attention_kernel, layer, heads, nope, la...  39.3 us

profile of v1, /device:TPU:0, one launch (start us, length us, event | category | flops | bytes accessed | tf_op | source)
XLA Modules:
  0.0 123.4 jit_solution(16652655440388719223)
XLA Ops:
  0.6 0.7 convert_element_type.10
  1.3 1.0 fusion.table_ref
  2.3 20.6 %attention.2 = (f32[128,2560]{1,0:T(8,128)}, bf16[128,288,256]{2,1,0:T(8,128)(2,1)}) custom-call(s32[128]{0:T(128)} %lengths.3, bf16[128,2560]{1,0:T(8,128)(2,1)} %x_in.1, f32[128,128]{1,0:T(8,128)} %fusion.table_ref, f32[2,2560]{1,0:T(2,128)} %attn_g.7, f32[2,256]{1,0:T(2,128)} %kv_g.7, f32[2,768]{1,0:T(2,128)} %q_g.7, bf16[128,288,256]{2,1,0:T(8,128)(2,1)} %bitcast.11, ...), custom_call_target="tpu_custom_call" | custom-call | tf_op jit(solution)/shard_map/attention/pallas_call | solution.py:208
  22.8 41.4 %ffn.2 = (bf16[128,1152]{1,0:T(8,128)(2,1)}, bf16[64,2560]{1,0:T(8,128)(2,1)}) custom-call(f32[128,2560]{1,0:T(8,128)} %get-tuple-element.11.part, bf16[128,2560]{1,0:T(8,128)(2,1)} %x_in.1, f32[128,128]{1,0:T(8,128)} %fusion.table_ref, f32[2,2560]{1,0:T(2,128)} %ffn_g.3, f32[2,2560]{1,0:T(2,128)} %attn_g.7, f32[2,256]{1,0:T(2,128)} %kv_g.7, f32[2,768]{1,0:T(2,128)} %q_g.7, ...), custom_call_target="tpu_custom_call" | custom-call | tf_op jit(solution)/shard_map/ffn/pallas_call | solution.py:378
  64.2 18.7 %attention.3 = (f32[128,2560]{1,0:T(8,128)}, bf16[128,288,256]{2,1,0:T(8,128)(2,1)}) custom-call(s32[128]{0:T(128)} %lengths.3, bf16[128,1152]{1,0:T(8,128)(2,1)} %get-tuple-element.12.given, f32[128,128]{1,0:T(8,128)} %fusion.table_ref, f32[2,2560]{1,0:T(2,128)} %attn_g.7, f32[2,256]{1,0:T(2,128)} %kv_g.7, f32[2,768]{1,0:T(2,128)} %q_g.7, ...), custom_call_target="tpu_custom_call" | custom-call | tf_op jit(solution)/shard_map/attention/pallas_call | solution.py:208
  83.0 38.1 %ffn.3 = (bf16[64,2560]{1,0:T(8,128)(2,1)}, bf16[64,2560]{1,0:T(8,128)(2,1)}) custom-call(f32[128,2560]{1,0:T(8,128)} %get-tuple-element.13.part, bf16[64,2560]{1,0:T(8,128)(2,1)} %get-tuple-element.14.x_in, f32[128,128]{1,0:T(8,128)} %fusion.table_ref, f32[2,2560]{1,0:T(2,128)} %ffn_g.3, f32[2,2560]{1,0:T(2,128)} %attn_g.7, f32[2,256]{1,0:T(2,128)} %kv_g.7, ...), custom_call_target="tpu_custom_call" | custom-call | tf_op jit(solution)/shard_map/ffn/pallas_call | solution.py:378
  121.1 2.3 %maximum_select_fusion = bf16[128,2560]{1,0:T(8,128)(2,1)} fusion(bf16[64,2560]{1,0:T(8,128)(2,1)} %get-tuple-element.16, bf16[64,2560]{1,0:T(8,128)(2,1)} %get-tuple-element.15, pred[]{:T(512)S(6)} %eq.6), kind=kLoop, calls=%fused_computation | loop fusion | flops 2949120 | bytes 1310721 | tf_op jit(solution)/shard_map/jit(_where)/select_n | solution.py:411
  (2 shorter events, 0.0 us)

commit v2 on v1

--- a/solution.py
+++ b/solution.py
@@ -17,8 +17,8 @@
 LANES = 128
 PITCH_PAD = 8
 HIDDEN_BLOCKS = 5
-HIDDEN_SLOTS = 3
 OUT_BLOCKS = 5
+PIECES = 4
 MESH = pl.DeviceIdType.MESH
 VMEM_LIMIT = 60 * 1024 * 1024
 
@@ -52,18 +52,18 @@
     return lax.dot_general(a, b, (((1,), (1,)), ((), ())), preferred_element_type=F32)
 
 
-def low_rank(x_rows, table, attn_g, kv_g, q_g, dkv, qa, out):
-    q_rank = qa.shape[1]
+def low_query(normed, q_g, qa, out):
+    out[...] = rms_norm(dot(normed, qa[...]), q_g)
+
+
+def low_entry(normed, table, kv_g, dkv, out):
     latent = kv_g.shape[1]
     width = dkv.shape[0]
-    rows = x_rows.shape[0]
-    normed = rms_norm(x_rows, attn_g)
-    out[:, 0:q_rank] = rms_norm(dot(normed, qa[...]), q_g)
     kv_lat = dot_nt(normed, dkv[...])
-    out[:, q_rank:q_rank + latent] = rms_norm(kv_lat[:, :latent], kv_g)
+    out[:, :latent] = rms_norm(kv_lat[:, :latent], kv_g)
     turned = rotate(kv_lat[:, latent:], table).astype(BF16)
-    pad = jnp.zeros((rows, out.shape[1] - q_rank - width), BF16)
-    out[:, q_rank + latent:] = jnp.concatenate([turned, pad], axis=1)
+    pad = jnp.zeros((normed.shape[0], out.shape[1] - width), BF16)
+    out[:, latent:] = jnp.concatenate([turned, pad], axis=1)
 
 
 def attention_kernel(layer, heads, nope, latent, lengths, given, table_ref, attn_g, kv_g, q_g, cache, w_dkv, w_qa, w_qb, w_uk, w_uv, w_o, part, new_cache,
@@ -102,7 +102,9 @@
     if first:
         load_weight(0).wait()
         load_weight(1).wait()
-        low_rank(given[...], table, attn_g[layer:layer + 1], kv_g[layer:layer + 1], q_g[layer:layer + 1], dkv, qa, low)
+        normed = rms_norm(given[...], attn_g[layer:layer + 1])
+        low_query(normed, q_g[layer:layer + 1], qa, low.at[:, :q_rank])
+        low_entry(normed, table, kv_g[layer:layer + 1], dkv, low.at[:, q_rank:])
     else:
         low = given
     entry[...] = low[:, q_rank:].astype(F32)
@@ -232,16 +234,17 @@
 def ffn_kernel(layer, last, part, x_in, table_ref, ffn_g, attn_g, kv_g, q_g, w_gate, w_up, w_down, w_dkv, w_qa, *rest):
     if last:
         out_own, out_far, *rest = rest
-        wides, downs, arrived, x_mid, g_pair, hidden, mine, outgoing, incoming, x_new, x_far, sems, dsem, ssem, rsem = rest
+        wides, downs, kept, ksem, arrived, x_mid, g_pair, hidden, mine, outgoing, incoming, x_new, x_far, sems, dsem, ssem, rsem = rest
     else:
         low_out, x_out, *rest = rest
-        wides, downs, arrived, x_mid, g_pair, hidden, mine, outgoing, incoming, low_mine, low_far, dkv, qa, sems, dsem, lsem, ssem, rsem = rest
+        wides, downs, kept, ksem, arrived, x_mid, g_pair, hidden, mine, outgoing, incoming, q_mine, q_far, kv_mine, kv_far, dkv, qa, sems, dsem, lsem, ssem, rsem = rest
     tp = lax.axis_index("tp")
     dp = lax.axis_index("dp")
     core = lax.rem(dp, 2)
     peer = {"tp": 1 - tp}
     mate = {"dp": dp + 1 - 2 * core}
     half, model = arrived.shape
+    h_slots = wides.shape[0]
     h_block = wides.shape[2] // 2
     h_width = hidden.shape[1]
     o_block = downs.shape[2]
@@ -255,7 +258,10 @@
     def down_load(c):
         return pltpu.make_async_copy(w_down.at[layer, pl.ds(pl.multiple_of(core * h_width, LANES), h_width), pl.ds(c * o_block, o_block)], downs.at[c], dsem.at[c])
 
-    for b in range(HIDDEN_SLOTS):
+    barrier = pltpu.get_barrier_semaphore()
+    for other in (peer, mate):
+        pl.semaphore_signal(barrier, inc=1, device_id=other, device_id_type=MESH)
+    for b in range(h_slots):
         for copy in hidden_loads(b, b):
             copy.start()
     for c in range(OUT_BLOCKS):
@@ -265,43 +271,53 @@
         for copy in loads:
             copy.start()
 
-    barrier = pltpu.get_barrier_semaphore()
-    for other in (peer, mate):
-        pl.semaphore_signal(barrier, inc=1, device_id=other, device_id_type=MESH)
     pl.semaphore_wait(barrier, 2)
 
     def send(src, dst, n, to):
         return pltpu.make_async_remote_copy(src_ref=src, dst_ref=dst, send_sem=ssem.at[n], recv_sem=rsem.at[n], device_id=to, device_id_type=MESH)
 
-    scatter = send(part.at[far], arrived, 0, peer)
-    scatter.start()
-    x_own = x_in[own, :] if layer == 0 else x_in[...]
-    scatter.wait_recv()
-    x_mid[...] = (x_own.astype(F32) + (part[own, :] + arrived[...])).astype(BF16)
-    g_pair[0:half, :] = rms_norm(x_mid[...], ffn_g[layer:layer + 1])
-    swap = send(g_pair.at[0:half], g_pair.at[half:2 * half], 1, mate)
-    swap.start()
-    swap.wait_recv()
+    keep = pltpu.make_async_copy(part.at[own], kept, ksem)
+    keep.start()
+    piece = half // PIECES
+    scatters, swaps = [], []
+    for n in range(PIECES):
+        rows = slice(n * piece, (n + 1) * piece)
+        start = pl.multiple_of((1 - tp) * half + n * piece, piece)
+        scatters.append(send(part.at[pl.ds(start, piece)], arrived.at[rows], n, peer))
+        swaps.append(send(g_pair.at[rows], g_pair.at[half + n * piece:half + (n + 1) * piece], PIECES + n, mate))
+        scatters[n].start()
+    keep.wait()
+    for n in range(PIECES):
+        rows = slice(n * piece, (n + 1) * piece)
+        mine_rows = pl.ds(pl.multiple_of(tp * half + n * piece, piece), piece)
+        x_own = x_in[mine_rows, :] if layer == 0 else x_in[rows, :]
+        scatters[n].wait_recv()
+        mid = (x_own.astype(F32) + (kept[rows, :] + arrived[rows, :])).astype(BF16)
+        x_mid[rows, :] = mid
+        g_pair[rows, :] = rms_norm(mid, ffn_g[layer:layer + 1])
+        swaps[n].start()
+    for n in range(PIECES):
+        swaps[n].wait_recv()
 
     def hidden_step(b, carry):
-        slot = lax.rem(b, HIDDEN_SLOTS)
+        slot = lax.rem(b, h_slots)
         for copy in hidden_loads(b, slot):
             copy.wait()
         both = dot(g_pair[...], wides[slot])
         gate, up = both[:, :h_block], both[:, h_block:]
         hidden[:, pl.ds(pl.multiple_of(b * h_block, LANES), h_block)] = (jax.nn.silu(gate) * up).astype(BF16)
 
-        @pl.when(b + HIDDEN_SLOTS < HIDDEN_BLOCKS)
+        @pl.when(b + h_slots < HIDDEN_BLOCKS)
         def _():
-            for copy in hidden_loads(b + HIDDEN_SLOTS, slot):
+            for copy in hidden_loads(b + h_slots, slot):
                 copy.start()
         return carry
 
     lax.fori_loop(0, HIDDEN_BLOCKS, hidden_step, 0)
 
-    returns = [send(outgoing.at[c], incoming.at[c], 2 + c, mate) for c in range(OUT_BLOCKS)]
+    returns = [send(outgoing.at[c], incoming.at[c], 2 * PIECES + c, mate) for c in range(OUT_BLOCKS)]
     if last:
-        spreads = [send(x_new.at[c], x_far.at[c], 2 + OUT_BLOCKS + c, peer) for c in range(OUT_BLOCKS)]
+        spreads = [send(x_new.at[c], x_far.at[c], 2 * PIECES + OUT_BLOCKS + c, peer) for c in range(OUT_BLOCKS)]
 
     def finish(c):
         returns[c].wait_recv()
@@ -333,15 +349,24 @@
         for copy in loads:
             copy.wait()
         nxt = layer + 1
-        low_rank(x_out[...], table_ref[own, :], attn_g[nxt:nxt + 1], kv_g[nxt:nxt + 1], q_g[nxt:nxt + 1], dkv, qa, low_mine)
-        share = send(low_mine, low_far, 2 + OUT_BLOCKS, peer)
-        share.start()
-        low_out[own, :] = low_mine[...]
-        share.wait_recv()
-        low_out[far, :] = low_far[...]
-        share.wait_send()
-    scatter.wait_send()
-    swap.wait_send()
+        q_rank = qa.shape[1]
+        shares = [send(a, b, 2 * PIECES + OUT_BLOCKS + n, peer) for n, (a, b) in enumerate(((q_mine, q_far), (kv_mine, kv_far)))]
+        normed = rms_norm(x_out[...], attn_g[nxt:nxt + 1])
+        low_query(normed, q_g[nxt:nxt + 1], qa, q_mine)
+        shares[0].start()
+        low_entry(normed, table_ref[own, :], kv_g[nxt:nxt + 1], dkv, kv_mine)
+        shares[1].start()
+        low_out[own, :q_rank] = q_mine[...]
+        low_out[own, q_rank:] = kv_mine[...]
+        shares[0].wait_recv()
+        low_out[far, :q_rank] = q_far[...]
+        shares[1].wait_recv()
+        low_out[far, q_rank:] = kv_far[...]
+        for share in shares:
+            share.wait_send()
+    for n in range(PIECES):
+        scatters[n].wait_send()
+        swaps[n].wait_send()
     for c in range(OUT_BLOCKS):
         returns[c].wait_send()
 
@@ -351,11 +376,14 @@
     half = rows // 2
     h_width = w_gate.shape[2] // 2
     h_block = h_width // HIDDEN_BLOCKS
+    h_slots = HIDDEN_BLOCKS if last else HIDDEN_BLOCKS - 1
     o_block = model // OUT_BLOCKS
     padded = low_width(w_qa, w_dkv_t)
     scratch = [
-        pltpu.VMEM((HIDDEN_SLOTS, model, 2 * h_block), BF16),
+        pltpu.VMEM((h_slots, model, 2 * h_block), BF16),
         pltpu.VMEM((OUT_BLOCKS, h_width, o_block), BF16),
+        pltpu.VMEM((half, model), F32),
+        pltpu.SemaphoreType.DMA(()),
         pltpu.VMEM((half, model), F32),
         pltpu.VMEM((half, model), BF16),
         pltpu.VMEM((rows, model), BF16),
@@ -368,17 +396,18 @@
     if last:
         out_shape = (jax.ShapeDtypeStruct((half, model), BF16),) * 2
         out_specs = (VMEM, VMEM)
-        scratch += [pltpu.VMEM((OUT_BLOCKS, half, o_block), BF16)] * 2 + [dma((2, HIDDEN_SLOTS)), dma((OUT_BLOCKS,))]
+        scratch += [pltpu.VMEM((OUT_BLOCKS, half, o_block), BF16)] * 2 + [dma((2, h_slots)), dma((OUT_BLOCKS,))]
     else:
         out_shape = (jax.ShapeDtypeStruct((rows, padded), BF16), jax.ShapeDtypeStruct((half, model), BF16))
         out_specs = (VMEM, VMEM)
-        scratch += [pltpu.VMEM((half, padded), BF16)] * 2 + [pltpu.VMEM(w_dkv_t.shape[1:], BF16), pltpu.VMEM(w_qa.shape[1:], BF16)]
-        scratch += [dma((2, HIDDEN_SLOTS)), dma((OUT_BLOCKS,)), dma((2,))]
-    copies = 2 + OUT_BLOCKS + (OUT_BLOCKS if last else 1)
+        q_rank = w_qa.shape[2]
+        scratch += [pltpu.VMEM((half, q_rank), BF16)] * 2 + [pltpu.VMEM((half, padded - q_rank), BF16)] * 2 + [pltpu.VMEM(w_dkv_t.shape[1:], BF16), pltpu.VMEM(w_qa.shape[1:], BF16)]
+        scratch += [dma((2, h_slots)), dma((OUT_BLOCKS,)), dma((2,))]
+    copies = 2 * PIECES + OUT_BLOCKS + (OUT_BLOCKS if last else 2)
     return pl.pallas_call(
         functools.partial(ffn_kernel, layer, last),
         out_shape=out_shape,
-        in_specs=[VMEM] * 7 + [ANY] * 5,
+        in_specs=[ANY] + [VMEM] * 6 + [ANY] * 5,
         out_specs=out_specs,
         scratch_shapes=scratch + [dma((copies,)), dma((copies,))],
         compiler_params=pltpu.CompilerParams(vmem_limit_bytes=VMEM_LIMIT, collective_id=layer, has_side_effects=True),

time: 124 us -> 119 us (0.960)
  Pallas kernels: 119 us -> 114 us
    pallas_call x2, Pallas kernels: 79.5 us -> 74.4 us  [ffn(): pl.pallas_call(functools.partial(ffn_kernel, layer, last), out_shape=out_...]
where the time goes in v2:
time: 119 us; the launch traced here: 118 us
  Pallas kernels  114 us (96%)
  other arithmetic  3.91 us (3%)
    pallas_call x2, Pallas kernels, ffn(): pl.pallas_call(functools.partial(ffn_kernel, layer, last), out_shape=out_...  74.4 us
    pallas_call x2, Pallas kernels, attention(): pl.pallas_call(functools.partial(attention_kernel, layer, heads, nope, la...  39.3 us

profile of v2, /device:TPU:0, one launch (start us, length us, event | category | flops | bytes accessed | tf_op | source)
XLA Modules:
  0.0 118.3 jit_solution(1192994746334380451)
XLA Ops:
  0.6 0.7 convert_element_type.10
  1.3 1.0 fusion.table_ref
  2.3 20.6 %attention.2 = (f32[128,2560]{1,0:T(8,128)}, bf16[128,288,256]{2,1,0:T(8,128)(2,1)}) custom-call(s32[128]{0:T(128)} %lengths.3, bf16[128,2560]{1,0:T(8,128)(2,1)} %x_in.1, f32[128,128]{1,0:T(8,128)} %fusion.table_ref, f32[2,2560]{1,0:T(2,128)} %attn_g.7, f32[2,256]{1,0:T(2,128)} %kv_g.7, f32[2,768]{1,0:T(2,128)} %q_g.7, bf16[128,288,256]{2,1,0:T(8,128)(2,1)} %bitcast.11, ...), custom_call_target="tpu_custom_call" | custom-call | tf_op jit(solution)/shard_map/attention/pallas_call | solution.py:210
  22.8 38.7 %ffn.2 = (bf16[128,1152]{1,0:T(8,128)(2,1)}, bf16[64,2560]{1,0:T(8,128)(2,1)}) custom-call(f32[128,2560]{1,0:T(8,128)} %get-tuple-element.11.part, bf16[128,2560]{1,0:T(8,128)(2,1)} %x_in.1, f32[128,128]{1,0:T(8,128)} %fusion.table_ref, f32[2,2560]{1,0:T(2,128)} %ffn_g.3, f32[2,2560]{1,0:T(2,128)} %attn_g.7, f32[2,256]{1,0:T(2,128)} %kv_g.7, f32[2,768]{1,0:T(2,128)} %q_g.7, ...), custom_call_target="tpu_custom_call" | custom-call | tf_op jit(solution)/shard_map/ffn/pallas_call | solution.py:407
  61.5 18.7 %attention.3 = (f32[128,2560]{1,0:T(8,128)}, bf16[128,288,256]{2,1,0:T(8,128)(2,1)}) custom-call(s32[128]{0:T(128)} %lengths.3, bf16[128,1152]{1,0:T(8,128)(2,1)} %get-tuple-element.12.given, f32[128,128]{1,0:T(8,128)} %fusion.table_ref, f32[2,2560]{1,0:T(2,128)} %attn_g.7, f32[2,256]{1,0:T(2,128)} %kv_g.7, f32[2,768]{1,0:T(2,128)} %q_g.7, ...), custom_call_target="tpu_custom_call" | custom-call | tf_op jit(solution)/shard_map/attention/pallas_call | solution.py:210
  80.3 35.7 %ffn.3 = (bf16[64,2560]{1,0:T(8,128)(2,1)}, bf16[64,2560]{1,0:T(8,128)(2,1)}) custom-call(f32[128,2560]{1,0:T(8,128)} %get-tuple-element.13.part, bf16[64,2560]{1,0:T(8,128)(2,1)} %get-tuple-element.14.x_in, f32[128,128]{1,0:T(8,128)} %fusion.table_ref, f32[2,2560]{1,0:T(2,128)} %ffn_g.3, f32[2,2560]{1,0:T(2,128)} %attn_g.7, f32[2,256]{1,0:T(2,128)} %kv_g.7, ...), custom_call_target="tpu_custom_call" | custom-call | tf_op jit(solution)/shard_map/ffn/pallas_call | solution.py:407
  116.0 2.3 %maximum_select_fusion = bf16[128,2560]{1,0:T(8,128)(2,1)} fusion(bf16[64,2560]{1,0:T(8,128)(2,1)} %get-tuple-element.16, bf16[64,2560]{1,0:T(8,128)(2,1)} %get-tuple-element.15, pred[]{:T(512)S(6)} %eq.6), kind=kLoop, calls=%fused_computation | loop fusion | flops 2949120 | bytes 1310721 | tf_op jit(solution)/shard_map/jit(_where)/select_n | solution.py:440
  (2 shorter events, 0.0 us)
